TPU v7x, 256 devices: a whole 4x4x8 slice. The times are simulated.
256 devices in a mesh: occ: 32 (over x, z_lo, core), aux: 8 (over y, z_hi).
Axes of the slice: x: 4, y: 4, z: 8 (z_hi: 2, z_lo: 4; z = z_hi * 4 + z_lo), core: 2. Of those that a mesh axis runs over, the one named last changes fastest.
Arguments:
- b_factors: bfloat16 [32, 256, 12288], P('occ', None, 'aux'), may hold values from -0.056884766 to 0.056884766
- occ_energies: float32 [32], P('occ'), may hold values from -1.2 to -0.3
- vir_energies: float32 [256], replicated, may hold values from 0.1 to 4
- pair_list: int32 [32, 48, 3], P('occ'), may hold values from -1 to 31, as said below
- pair_count: int32 [32], P('occ'), may hold values from 1 to 48, as said below
Outputs:
- pair_energy: float32 [32, 48], P('occ', 'aux')
- total_energy: float32 [], replicated
Inputs may be any that keep to these rules, and one draw needn't show every extreme that they name: `pair_list`: row i lists pair_count[i] distinct items (j, a-block, b-block) with j in 0 to 31 and blocks in 0 to 1, ordered by j, then a-block, then b-block; its other slots hold -1 in all three fields. `pair_count`: some occupied orbital lists exactly 48 items.
All inputs are finite; a program needn't handle non-finite values.
Results may differ from a plain program's by a relative error of at most 0.0003.
Values may be sent and summed in bfloat16 or wider, within the bound.
A program may use at most 128 MiB of HBM per device.

v0:
```python
import jax
import jax.numpy as jnp
from jax import lax
from jax.sharding import Mesh
from jax.sharding import PartitionSpec as P

VB = 128
OCC = ("occ_0", "occ_1", "occ_2")
AUX = ("aux_0", "aux_1")
OCC_AUX = ("occ_0", "occ_1", "occ_2", "aux_0", "aux_1")


def joined_along(pieces, dim):
    pieces = jnp.moveaxis(pieces, 0, dim)
    lengths = pieces.shape
    return pieces.reshape(*lengths[:dim], lengths[dim] * lengths[dim + 1], *lengths[dim + 2 :])


def sent_to_all(array, axis):
    count = lax.axis_size(axis)
    return lax.all_to_all(
        jnp.broadcast_to(array[None], (count, *array.shape)), axis, 0, 0, tiled=True
    )


def gathered_copies(array, axis, dim):
    return joined_along(sent_to_all(array, axis), dim)


def summed_rows(array, axes, dim):
    for axis in axes:
        array = lax.psum_scatter(array, axis, scatter_dimension=dim, tiled=True)
    return array


def by_axis(array, axes):
    for axis in axes:
        array = lax.psum(array, axis)
    return array


def local(b_factors, occ_energies, vir_energies, pair_list, pair_count):
    home_panel = b_factors[0]
    item_table = pair_list[0]
    slot_count = pair_count[0]
    slot_total = item_table.shape[0]
    virt_width = home_panel.shape[0]
    block_count = virt_width // VB
    live_slots = jnp.arange(slot_total, dtype=jnp.int32) < slot_count
    all_occ = gathered_copies(occ_energies, OCC, 0)
    cycle_width = lax.axis_size(OCC)
    shard_rows = b_factors.shape[0]
    orbital_total = cycle_width * shard_rows
    contract = (((1,), (2,)), ((), ()))
    block = lax.dot_general(
        home_panel,
        lax.all_gather(b_factors, OCC, axis=0, tiled=True),
        contract,
        preferred_element_type=jnp.float32,
    )
    block = jnp.transpose(block, (1, 0, 2))
    tiles = block.reshape(orbital_total, block_count, VB, block_count, VB)
    tiles = jnp.transpose(tiles, (0, 1, 3, 2, 4)).reshape(
        orbital_total * block_count * block_count, VB, VB
    )
    partner_ids = jnp.maximum(item_table[:, 0], 0)
    left_ids = jnp.maximum(item_table[:, 1], 0)
    right_ids = jnp.maximum(item_table[:, 2], 0)
    direct_code = (partner_ids * block_count + left_ids) * block_count + right_ids
    swapped_code = (partner_ids * block_count + right_ids) * block_count + left_ids
    direct_tiles = jnp.take(tiles, direct_code, axis=0)
    swapped_tiles = jnp.take(tiles, swapped_code, axis=0)
    tile_stack = jnp.stack([direct_tiles, swapped_tiles], axis=1)
    reduced = summed_rows(tile_stack, AUX, 0)
    aux_width = lax.axis_size(AUX)
    per_device = slot_total // aux_width
    share_start = lax.axis_index(AUX) * per_device
    my_items = lax.dynamic_slice_in_dim(item_table, share_start, per_device, 0)
    my_live = lax.dynamic_slice_in_dim(live_slots, share_start, per_device, 0)
    block_ids = jnp.arange(block_count, dtype=jnp.int32)
    virtual_blocks = vir_energies.reshape(block_count, VB)
    picks_left = (my_items[:, 1][:, None] == block_ids[None, :]).astype(jnp.float32)
    picks_right = (my_items[:, 2][:, None] == block_ids[None, :]).astype(jnp.float32)
    left_energy = jnp.dot(picks_left, virtual_blocks, precision=lax.Precision.HIGHEST)
    right_energy = jnp.dot(picks_right, virtual_blocks, precision=lax.Precision.HIGHEST)
    orbital_ids = jnp.arange(all_occ.shape[0], dtype=jnp.int32)
    partner_energy = jnp.sum(
        jnp.where(my_items[:, 0][:, None] == orbital_ids[None, :], all_occ[None, :], 0.0), axis=1
    )
    denominator = (
        left_energy[:, :, None]
        + right_energy[:, None, :]
        - occ_energies[0]
        - partner_energy[:, None, None]
    )
    direct = reduced[:, 0]
    swapped_back = jnp.transpose(reduced[:, 1], (0, 2, 1))
    energy = -jnp.sum(direct * (2.0 * direct - swapped_back) / denominator, axis=(1, 2))
    energy = jnp.where(my_live, energy, jnp.zeros_like(energy))
    total_energy = by_axis(jnp.sum(energy), OCC_AUX)
    return (energy[None, :], total_energy)


def solution(mesh):
    finer = Mesh(mesh.devices.reshape(4, 4, 2, 4, 2), ("occ_0", "occ_1", "occ_2", "aux_0", "aux_1"))
    placed = (P(OCC, None, AUX), P(OCC), P(), P(OCC, None, None), P(OCC))
    return jax.shard_map(
        local, mesh=finer, in_specs=placed, out_specs=(P(OCC, AUX), P()), check_vma=False
    )
```

profile of v0, /device:TPU:1, one launch (start us, length us, event | category | flops | bytes accessed | tf_op | source)
XLA Modules:
  0.0 491.8 jit_solution(6576529788671518339)
XLA Ops:
  7.2 0.0 copy-start
  7.2 0.0 all-gather.2.cloned.1.call-start
  7.2 0.7 all-gather.2.cloned.1.call-update
  7.9 0.0 all-reduce.5.cloned.1.call-start
  8.0 0.7 copy.26
  8.7 147.3 %all-gather.2.cloned.1.call-done = bf16[32,256,1536]{2,1,0:T(8,128)(2,1)} async-done(((bf16[1,256,1536]{2,1,0:T(8,128)(2,1)}), bf16[32,256,1536]{2,1,0:T(8,128)(2,1)}) %all-gather.2.cloned.1.call-update) | async-done | bytes 25165840 | tf_op jit(solution)/shard_map/all_gather | solution.py:57
  156.0 13.8 %convolution_bitcast_fusion = f32[32,256,256]{2,1,0:T(8,128)} fusion(bf16[32,256,1536]{2,1,0:T(8,128)(2,1)} %all-gather.2.cloned.1.call-done, bf16[1,256,1536]{2,1,0:T(8,128)(2,1)} %param.7), kind=kOutput, calls=%fused_computation.3 | convolution fusion | flops 6442450944 | bytes 34340864 | tf_op jit(solution)/shard_map/dot_general | solution.py:55
  169.7 10.8 %reshape.37 = f32[32,2,128,2,128]{4,3,2,1,0:T(2,128)} reshape(f32[32,256,256]{2,1,0:T(8,128)} %convolution_bitcast_fusion) | data formatting | bytes 16777216 | tf_op jit(solution)/shard_map/reshape | solution.py:62
  180.5 7.8 %copy.14 = f32[32,2,128,2,128]{4,2,3,1,0:T(8,128)} copy(f32[32,2,128,2,128]{4,3,2,1,0:T(2,128)} %reshape.37) | data formatting | bytes 16777216 | tf_op jit(solution)/shard_map/reshape | solution.py:62
  188.3 4.1 gather_fusion.1
  192.4 5.8 %gather_fusion = f32[48,128,128]{2,1,0:T(8,128)} fusion(f32[128,128,128]{2,1,0:T(8,128)} %bitcast.102, s32[1024]{0:T(1024)S(1)} %pad_clamp_fusion.1), kind=kCustom, calls=%fused_computation.clone | custom fusion | bytes 6291648 | tf_op jit(solution)/shard_map/jit(_take)/gather | solution.py:71
  198.2 2.4 select_bitcast_fusion
  200.6 3.4 pad_maximum_fusion
  204.0 0.0 copy-start.3
  204.0 0.0 all-reduce.5.cloned.1.call-update
  204.0 0.0 copy-start.2
  204.0 0.0 copy-start.1
  204.0 0.0 all-reduce.7.cloned.1.call-start
  204.1 0.6 copy-done.3
  204.7 0.6 dynamic-slice.1
  205.9 130.5 %all-reduce.5.cloned.1.call-done = f32[48,2,128,128]{3,2,0,1:T(8,128)} async-done(((f32[48,2,128,128]{3,2,0,1:T(8,128)}), f32[48,2,128,128]{3,2,0,1:T(8,128)}) %all-reduce.5.cloned.1.call-update) | async-done | bytes 6291472
  336.4 2.7 constant_dynamic-slice_fusion.1
  339.1 0.0 all-reduce.7.cloned.1.call-update
  339.8 0.6 broadcast_in_dim.38
  340.4 8.2 %all-to-all-start = ((f32[32,1,1]{2,1,0:T(1,128)}), f32[32,1,1]{2,1,0:T(1,128)S(1)}, u32[]{:S(2)}, u32[]{:S(2)}) async-start(f32[32,1,1]{2,1,0:T(1,128)} %broadcast_in_dim.38), calls=%async_computation | async-start | bytes 32768 | tf_op jit(solution)/shard_map/all_to_all | solution.py:21
  348.6 0.0 copy-done.2
  348.6 0.6 dynamic-slice.3
  349.2 0.0 copy-done.1
  349.2 0.1 constant_dynamic-slice_fusion.2
  350.0 0.0 copy-done
  350.0 0.2 fusion.6
  350.2 0.2 fusion.5
  351.0 4.8 all-to-all-done
  355.8 0.3 reduce
  356.1 0.2 select_reduce_fusion
  356.3 83.8 %all-reduce.7.cloned.1.call-done = f32[12,2,128,128]{3,2,0,1:T(8,128)} async-done(((f32[12,2,128,128]{3,2,0,1:T(8,128)}), f32[12,2,128,128]{3,2,0,1:T(8,128)}) %all-reduce.7.cloned.1.call-update) | async-done | bytes 1572880
  440.1 1.0 constant_dynamic-slice_fusion
  441.2 0.2 copy.22
  441.3 1.3 fusion.4
  442.6 1.2 fusion.14
  443.8 9.0 %psum.35 = f32[]{:T(128)} all-reduce(f32[]{:T(128)} %get-tuple-element.3), channel_id=1, replica_groups=mesh['occ_0'=4,'occ_1'=4,'occ_2'=2,'aux_0'=4,'aux_1'=2] {'occ_0'}, use_global_device_ids=true, to_apply=%region_5.7 | all-reduce | flops 1 | bytes 8 | tf_op jit(solution)/shard_map/psum | solution.py:38
  452.8 7.6 %psum.36 = f32[]{:T(128)} all-reduce(f32[]{:T(128)} %psum.35), channel_id=1, replica_groups=mesh['occ_0'=4,'occ_1'=4,'occ_2'=2,'aux_0'=4,'aux_1'=2] {'occ_1'}, use_global_device_ids=true, to_apply=%region_6.8 | all-reduce | flops 1 | bytes 8 | tf_op jit(solution)/shard_map/psum | solution.py:38
  460.4 7.5 %psum.37 = f32[]{:T(128)} all-reduce(f32[]{:T(128)} %psum.36), channel_id=1, replica_groups=mesh['occ_0'=4,'occ_1'=4,'occ_2'=2,'aux_0'=4,'aux_1'=2] {'occ_2'}, use_global_device_ids=true, to_apply=%region_7.9 | all-reduce | flops 1 | bytes 8 | tf_op jit(solution)/shard_map/psum | solution.py:38
  467.9 9.1 %psum.38 = f32[]{:T(128)} all-reduce(f32[]{:T(128)} %psum.37), channel_id=1, replica_groups=mesh['occ_0'=4,'occ_1'=4,'occ_2'=2,'aux_0'=4,'aux_1'=2] {'aux_0'}, use_global_device_ids=true, to_apply=%region_8.10 | all-reduce | flops 1 | bytes 8 | tf_op jit(solution)/shard_map/psum | solution.py:38
  476.9 8.3 %psum.39 = f32[]{:T(128)} all-reduce(f32[]{:T(128)} %psum.38), channel_id=1, replica_groups=mesh['occ_0'=4,'occ_1'=4,'occ_2'=2,'aux_0'=4,'aux_1'=2] {'aux_1'}, use_global_device_ids=true, to_apply=%region_9.11 | all-reduce | flops 1 | bytes 8 | tf_op jit(solution)/shard_map/psum | solution.py:38
  (6 shorter events, 0.0 us)
Async XLA Ops:
  7.2 342.8 %copy-start = (f32[256]{0:T(256)S(1)}, f32[256]{0:T(256)}, u32[]{:S(2)}) copy-start(f32[256]{0:T(256)} %param.9) | copy-start | bytes 3076
  7.2 148.8 %all-gather.2.cloned.1.call-start = ((), (), s32[]{:S(2)}) async-start(), calls=%async_computation.1 | async-start | bytes 25952256 | tf_op jit(solution)/shard_map/all_gather | solution.py:57
  7.9 328.5 %all-reduce.5.cloned.1.call-start = ((), (), s32[]{:S(2)}) async-start(), calls=%async_computation.2 | async-start | bytes 12582912
  204.0 0.7 copy-start.3
  204.0 144.6 %copy-start.2 = (u32[256]{0:T(256)S(1)}, u32[256]{0:T(256)}, u32[]{:S(2)}) copy-start(u32[256]{0:T(256)} %constant.44) | copy-start | bytes 3076
  204.0 145.2 %copy-start.1 = (s32[1,48,3]{1,0,2:T(1,128)S(1)}, s32[1,48,3]{1,0,2:T(1,128)}, u32[]{:S(2)}) copy-start(s32[1,48,3]{1,0,2:T(1,128)} %param.10) | copy-start | bytes 1732
  204.0 236.1 %all-reduce.7.cloned.1.call-start = ((), (), s32[]{:S(2)}) async-start(), calls=%async_computation.3 | async-start | bytes 3145728
  340.4 15.4 %all-to-all-start = ((f32[32,1,1]{2,1,0:T(1,128)}), f32[32,1,1]{2,1,0:T(1,128)S(1)}, u32[]{:S(2)}, u32[]{:S(2)}) async-start(f32[32,1,1]{2,1,0:T(1,128)} %broadcast_in_dim.38), calls=%async_computation | async-start | bytes 32768 | tf_op jit(solution)/shard_map/all_to_all | solution.py:21
Sparse Core Ops, SparseCore 0:
  9.8 146.0 all-gather.1
  204.1 132.2 all-reduce.4
  339.2 100.8 all-reduce.6
where the time goes:
time: 494 us; the launch traced here: 492 us
  waiting for transfers between devices  367 us (74%)
  blocking collectives  41.4 us (8%)
  local copies, waits for them, and re-layouts  35.5 us (7%)
  between operations  16.5 us (3%)
  matrix products  14.1 us (3%)
  other arithmetic  8.77 us (2%)
  starting transfers between devices  8.34 us (2%)
    unnamed x5, waiting for transfers between devices  215 us
    all_gather x1, waiting for transfers between devices, local(): lax.all_gather(b_factors, OCC, axis=0, tiled=True)  147 us
    psum x5, blocking collectives, by_axis(): array = lax.psum(array, axis)  41.4 us
    reshape x2, local copies, waits for them, and re-layouts, local(): tiles = block.reshape(orbital_total, block_count, VB, block_count, VB)  18.5 us
    dot_general x1, matrix products, local(): lax.dot_general(home_panel, lax.all_gather(b_factors, OCC, axis=0, tiled=...  13.8 us
  transfers between devices with their start and end apart: 4, of which 4 were waited for; matrix products, arithmetic and copies ran while one was open for 1% of the time, Pallas kernels for 0%

commit v1 on v0

v1 whole, which is shorter than its diff:
```python
import jax
import jax.numpy as jnp
from jax import lax
from jax.experimental import pallas as pl
from jax.experimental.pallas import tpu as pltpu
from jax.sharding import Mesh
from jax.sharding import PartitionSpec as P

VB = 128
NV = 256
NOCC = 32
SLOTS = 16
LOW = SLOTS - 1
HALF = 128
OCC = ("occ_0", "occ_1", "occ_2")
AUX = ("aux_0", "aux_1")
NAMES = ("occ_0", "occ_1", "occ_2", "aux_0", "aux_1")
MESH = pl.DeviceIdType.MESH

UNITS = (
    ((0, 0), (0, 1), (0, 2)),
    ((0, 0), (0, 1), (1, 0), (1, 1), (1, 3), (0, 2), (1, 2)),
    ((0, 0), (0, 1), (1, 0), (1, 1), (1, 3), (2, 0), (2, 1), (2, 3),
     (0, 2), (1, 2), (2, 2), (3, 0), (3, 1), (3, 3), (3, 2)),
    ((0, 0), (0, 1), (1, 0), (1, 1), (1, 3), (0, 2), (1, 2), (3, 0), (3, 1), (3, 3), (3, 2)),
)
COUNT = (3, 7, 15, 11)
SECOND = (2, 5, 8, 5)
THIRD = (3, 7, 11, 7)
ROW_AT = ((0, 1, 3, 3), (-1, 0, 1, 1), (-1, -1, 0, -1), (-1, -1, 2, 0))


def packed(values):
    total = 0
    for place, value in enumerate(values):
        total += value * 4**place
    return total


U_TABLE = tuple(packed([u for u, _ in row]) for row in UNITS)
DX_TABLE = tuple(packed([dx for _, dx in row]) for row in UNITS)


def kernel(b_hbm, info_out, codes, vir, out, panels, info_in, parts, relay_out, relay_in, fin_out, fin_in,
           keep, hx_out, hx_in, vsum, acc, first_in, all_out, all_in,
           load_sem, x_send, x_recv, d_send, d_recv, z_send, z_recv, relay_send, relay_recv,
           fin_send, fin_recv, hx_send, hx_recv, tail_send, tail_recv):
    x, z, c, y, h = (lax.axis_index(name) for name in NAMES)
    me = (x * 4 + z) * 2 + c
    xs, zs, ys = ([(v + k) % 4 for k in range(4)] for v in (x, z, y))
    cs, hs = (c, 1 - c), (h, 1 - h)
    at_least_one = (z + 3) // 4
    at_least_two = z // 2
    at_three = z // 3

    def by_z(table):
        steps = [table[k + 1] - table[k] for k in range(3)]
        return table[0] + steps[0] * at_least_one + steps[1] * at_least_two + steps[2] * at_three

    x_next, x_prev, y_next, y_prev = xs[1], xs[3], ys[1], ys[3]
    dev_x = ((x_next, z, c, y, h), (x_prev, z, c, y, h))
    dev_y = ((x, z, c, y_next, h), (x, z, c, y_prev, h))
    dev_core = (x, z, 1 - c, y, h)
    dev_h = (x, z, c, y, 1 - h)

    others = []
    for k in range(1, NOCC):
        kx, kz, kc = k // 8, k // 2 % 4, k % 2
        there = (-kx % 4 * 4 + -kz % 4) * 2 + kc
        others.append((k, there, (xs[kx], zs[kz], cs[kc], y, h), (xs[kx] * 4 + zs[kz]) * 2 + cs[kc]))
    aux_others = []
    for k in range(1, 8):
        ky, kh = k // 2, k % 2
        aux_others.append((k, -ky % 4 * 2 + kh, (x, z, c, ys[ky], hs[kh])))

    def send(src, dst, send_sem, recv_sem, device):
        return pltpu.make_async_remote_copy(
            src_ref=src, dst_ref=dst, send_sem=send_sem, recv_sem=recv_sem,
            device_id=device, device_id_type=MESH)

    def wait_in(dst, recv_sem):
        send(dst, dst, x_send.at[0], recv_sem, dev_core).wait_recv()

    def wait_out(src, send_sem):
        send(src, src, send_sem, x_recv.at[0], dev_core).wait_send()

    def half(slot, part):
        return panels.at[slot, pl.ds(part * HALF, HALF)]

    load = pltpu.make_async_copy(b_hbm.at[0], panels.at[0], load_sem)
    load.start()

    barrier = pltpu.get_barrier_semaphore()

    for _, _, device, _ in others:
        pl.semaphore_signal(barrier, inc=1, device_id=device, device_id_type=MESH)
    for _, _, device in aux_others:
        pl.semaphore_signal(barrier, inc=1, device_id=device, device_id_type=MESH)
    load.wait()
    pl.semaphore_wait(barrier, NOCC - 1 + 7)

    own_x = (
        send(half(0, 0), half(3, 0), x_send.at[0], x_recv.at[0], dev_x[0]),
        send(half(0, 1), half(3, 1), x_send.at[1], x_recv.at[1], dev_x[0]),
        send(half(0, 1), half(1, 1), x_send.at[2], x_recv.at[2], dev_x[1]),
        send(half(0, 0), half(1, 0), x_send.at[3], x_recv.at[3], dev_x[1]),
    )
    passed_x = (
        send(half(3, 0), half(2, 0), x_send.at[4], x_recv.at[4], dev_x[0]),
        send(half(1, 1), half(2, 1), x_send.at[5], x_recv.at[5], dev_x[1]),
    )

    def core_copy(dx):
        return send(panels.at[dx], panels.at[4 + dx], d_send.at[dx], d_recv.at[dx], dev_core)

    def z_copy(slot, to_slot, part, to_z, kind):
        return send(half(slot, part), half(to_slot, part), z_send.at[kind, part],
                    z_recv.at[to_slot - 7, part], (x, to_z, c, y, h))

    own_z = {0: (0, 8, 1), 1: (0, 8, 2), 3: (0, 9, 2)}
    own_x[0].start()
    own_x[2].start()
    for from_z, (slot, to_slot, to_z) in own_z.items():
        @pl.when(z == from_z)
        def _(slot=slot, to_slot=to_slot, to_z=to_z):
            z_copy(slot, to_slot, 0, to_z, 0).start()
            z_copy(slot, to_slot, 1, to_z, 0).start()
    core_copy(0).start()
    own_x[1].start()
    own_x[3].start()

    for _, there, device, index in others:
        send(info_out.at[index], info_in.at[there], tail_send.at[0], tail_recv.at[0], device).start()
    info_in[0] = info_out[me]
    acc[...] = jnp.zeros_like(acc)

    wait_in(panels.at[4], d_recv.at[0])

    row_of = lax.broadcasted_iota(jnp.int32, (VB, VB), 0)
    lane_of = lax.broadcasted_iota(jnp.int32, (VB, VB), 1)
    left = vir[0:1, :]
    right = vir[1:2, :]

    def as_column(row_values, shift):
        wide = jnp.broadcast_to(row_values, (VB, VB))
        return jnp.sum(jnp.where(lane_of == shift, wide, 0.0), axis=1, keepdims=True)

    @pl.when(y == 0)
    def _():
        vsum[...] = as_column(left, row_of) + left

    @pl.when(y == 1)
    def _():
        vsum[...] = as_column(right, row_of) + right

    @pl.when(y == 2)
    def _():
        vsum[...] = as_column(left, row_of % 64) + right

    @pl.when(y == 3)
    def _():
        vsum[...] = as_column(left, row_of % 64 + 64) + right

    count = by_z(COUNT)
    second = by_z(SECOND)
    third = by_z(THIRD)

    def low_part(value):
        return (value - value.astype(jnp.bfloat16).astype(jnp.float32)).astype(jnp.bfloat16)

    def products(n, u, dx):
        row_slot = (7 + u) * ((u + 3) // 4)
        rows = panels[row_slot]
        for dc in range(2):
            block = lax.dot_general(rows, panels[dc * 4 + dx], (((1,), (1,)), ((), ())),
                                    preferred_element_type=jnp.float32)
            upper = block[:VB, VB:]
            lower = block[VB:, :VB].T
            parts[n, dc, 0] = block[:VB, :VB]
            parts[n, dc, 1] = block[VB:, VB:]
            parts[n, dc, 2, 0:64] = upper[:64]
            parts[n, dc, 2, 64:128] = lower[:64]
            parts[n, dc, 3, 0:64] = upper[64:]
            parts[n, dc, 3, 64:128] = lower[64:]
        far = ys[2]
        for dc in range(2):
            relay_out[n, dc] = parts[n, dc, far].astype(jnp.bfloat16)
            send(relay_out.at[n, dc], relay_in.at[n, dc], relay_send.at[n, dc], relay_recv.at[n, dc],
                 dev_y[dc]).start()

        @pl.when(n == 0)
        def _():
            relay_out[LOW, 0] = low_part(parts[0, 0, far])
            send(relay_out.at[LOW, 0], relay_in.at[LOW, 0], relay_send.at[LOW, 0], relay_recv.at[LOW, 0],
                 dev_y[0]).start()

    def pass_on_low():
        wait_in(relay_in.at[LOW, 0], relay_recv.at[LOW, 0])
        parts[0, 0, y_next] += relay_in[LOW, 0].astype(jnp.float32)
        fin_out[LOW, 0, 0] = low_part(parts[0, 0, y_next] + relay_in[0, 0].astype(jnp.float32))
        fin_out[LOW, 1, 0] = low_part(parts[0, 0, y_prev])
        for way in range(2):
            send(fin_out.at[LOW, way, 0], fin_in.at[LOW, way, 0], fin_send.at[LOW, way], fin_recv.at[LOW, way],
                 dev_y[way]).start()

    def pass_on(n):
        for dc in range(2):
            wait_in(relay_in.at[n, dc], relay_recv.at[n, dc])

        @pl.when(n == 0)
        def _():
            pass_on_low()

        fin_out[n, 0, 0] = (parts[n, 0, y_next] + relay_in[n, 0].astype(jnp.float32)).astype(jnp.bfloat16)
        fin_out[n, 0, 1] = parts[n, 1, y_next].astype(jnp.bfloat16)
        fin_out[n, 1, 0] = parts[n, 0, y_prev].astype(jnp.bfloat16)
        fin_out[n, 1, 1] = (parts[n, 1, y_prev] + relay_in[n, 1].astype(jnp.float32)).astype(jnp.bfloat16)
        for way in range(2):
            send(fin_out.at[n, way], fin_in.at[n, way], fin_send.at[n, way], fin_recv.at[n, way],
                 dev_y[way]).start()

    def cross(n):
        def summed(dc):
            return parts[n, dc, y] + fin_in[n, 0, dc].astype(jnp.float32) + fin_in[n, 1, dc].astype(jnp.float32)

        for way in range(2):
            wait_in(fin_in.at[n, way], fin_recv.at[n, way])

        @pl.when(n == 0)
        def _():
            for way in range(2):
                wait_in(fin_in.at[LOW, way, 0], fin_recv.at[LOW, way])
                parts[0, 0, y] += fin_in[LOW, way, 0].astype(jnp.float32)

            @pl.when(h == 1)
            def _():
                hx_out[LOW] = low_part(summed(0))
                send(hx_out.at[LOW], hx_in.at[LOW], hx_send.at[LOW], hx_recv.at[LOW], dev_h).start()

        hx_out[n] = summed(1 - h).astype(jnp.bfloat16)
        send(hx_out.at[n], hx_in.at[n], hx_send.at[n], hx_recv.at[n], dev_h).start()
        keep[n] = summed(h)

    lane_row = lax.broadcasted_iota(jnp.int32, (1, VB), 1)

    def energies(n, u, dx):
        wait_in(hx_in.at[n], hx_recv.at[n])

        @pl.when(n == 0)
        def _():
            @pl.when(h == 0)
            def _():
                wait_in(hx_in.at[LOW], hx_recv.at[LOW])
                keep[0] += hx_in[LOW].astype(jnp.float32)

        tile = keep[n] + hx_in[n].astype(jnp.float32)
        u_three = u // 3
        u_two = u // 2 - u_three
        u_one = (u + 3) // 4 - u // 2
        row_z = z * (1 - (u + 3) // 4) + u_one * at_least_two + u_two * 3
        row_energy = info_in[(row_z - z + 4) % 4 * 2][1:2, :]
        column_energy = info_in[dx * 8 + h][1:2, :]
        denominator = vsum[...] - row_energy - column_energy
        lane = u * 32 + (h * 4 + dx) * 4

        @pl.when(y < 2)
        def _():
            value = -jnp.sum(tile * (2.0 * tile - tile.T) / denominator, axis=0, keepdims=True)
            value = jnp.sum(value, axis=1, keepdims=True)
            acc[0:1, :] += jnp.where(lane_row == lane + 3 * y, value, 0.0)

        @pl.when(y >= 2)
        def _():
            top, bottom, under = tile[:64], tile[64:], denominator[:64]
            value = -jnp.sum(top * (2.0 * top - bottom) / under, axis=0, keepdims=True)
            other = -jnp.sum(bottom * (2.0 * bottom - top) / under, axis=0, keepdims=True)
            value = jnp.sum(value, axis=1, keepdims=True)
            other = jnp.sum(other, axis=1, keepdims=True)
            acc[0:1, :] += jnp.where(lane_row == lane + 1, value, 0.0) + jnp.where(lane_row == lane + 2, other, 0.0)

    def pass_rows(part, slot, to_slot, to_z, kind):
        wait_in(half(slot, part), z_recv.at[slot - 7, part])
        z_copy(slot, to_slot, part, to_z, kind).start()

    def first_arrivals():
        own_x[0].wait_recv()
        passed_x[0].start()
        own_x[2].wait_recv()
        passed_x[1].start()
        for part in range(2):
            @pl.when(z == 1)
            def _():
                pass_rows(part, 8, 10, 2, 1)

            @pl.when(z == 2)
            def _():
                pass_rows(part, 8, 8, 3, 1)

            if part == 0:
                own_x[1].wait_recv()
                core_copy(3).start()
                own_x[3].wait_recv()
                core_copy(1).start()
        wait_in(panels.at[7], d_recv.at[3])
        wait_in(panels.at[5], d_recv.at[1])

    def second_arrivals():
        passed_x[0].wait_recv()
        passed_x[1].wait_recv()
        core_copy(2).start()

        @pl.when(z == 2)
        def _():
            pass_rows(0, 10, 10, 3, 2)

        wait_in(panels.at[6], d_recv.at[2])

    def third_arrivals():
        @pl.when(z == 2)
        def _():
            pass_rows(1, 10, 10, 3, 2)

        @pl.when(z == 3)
        def _():
            for part in range(2):
                wait_in(half(10, part), z_recv.at[3, part])

    def each(low, high, action):
        def one(n, carry):
            action(n)
            return carry

        lax.fori_loop(low, high, one, 0)

    def step(n, carry):
        u_table, dx_table = carry
        products(n, u_table % 4, dx_table % 4)

        @pl.when(n == 0)
        def _():
            pass_on(0)
            first_arrivals()

        @pl.when(n == second - 1)
        def _():
            each(1, second, pass_on)
            second_arrivals()

        @pl.when(n == 1)
        def _():
            cross(0)

            @pl.when(z == 3)
            def _():
                for part in range(2):
                    wait_in(half(8, part), z_recv.at[1, part])

        @pl.when(n == 4)
        def _():
            @pl.when(z == 2)
            def _():
                for part in range(2):
                    wait_in(half(9, part), z_recv.at[2, part])

        @pl.when(n == third - 1)
        def _():
            @pl.when(z >= 2)
            def _():
                each(1, early, cross)
                third_arrivals()

        return (u_table // 4, dx_table // 4)

    start = jnp.int32(0)
    early = (second + 1) // 2
    crossed = 1 + (early - 1) * at_least_two
    lax.fori_loop(0, count, step, (start + by_z(U_TABLE), start + by_z(DX_TABLE)))
    each(second, count, pass_on)
    each(crossed, count, cross)
    wait_in(info_in.at[pl.ds(1, NOCC - 1)], tail_recv.at[0])

    def finish(n, carry):
        u_table, dx_table = carry
        energies(n, u_table % 4, dx_table % 4)
        return (u_table // 4, dx_table // 4)

    lax.fori_loop(0, count, finish, (start + by_z(U_TABLE), start + by_z(DX_TABLE)))

    for _, there, device in aux_others:
        send(acc, first_in.at[there], tail_send.at[1], tail_recv.at[1], device).start()
    weights = jnp.zeros((1, VB), jnp.float32)
    for k in range(NOCC):
        weights += info_in[k, 0:1, :]
    wait_in(first_in.at[pl.ds(1, 7)], tail_recv.at[1])
    mine = acc[0:1, :]
    for k in range(1, 8):
        mine += first_in[k, 0:1, :]
    all_out[0:1, :] = mine
    all_out[1:2, :] = mine * weights

    for _, there, device, _ in others:
        send(all_out, all_in.at[there], tail_send.at[2], tail_recv.at[2], device).start()
    wanted = codes[...]
    lanes = lax.broadcasted_iota(jnp.int32, (8, VB), 1)
    picked = jnp.where(wanted == me * VB + lanes, all_out[0:1, :], 0.0)
    total = all_out[1:2, :]

    for k in range(4):
        own_x[k].wait_send()
    for k in range(2):
        passed_x[k].wait_send()
    for dx in range(4):
        core_copy(dx).wait_send()
    for part in range(2):
        @pl.when(z != 2)
        def _():
            wait_out(half(0, part), z_send.at[0, part])

        @pl.when(z == 1)
        def _():
            wait_out(half(8, part), z_send.at[1, part])

        @pl.when(z == 2)
        def _():
            wait_out(half(8, part), z_send.at[1, part])
            wait_out(half(10, part), z_send.at[2, part])

    def sent(n, carry):
        for k in range(2):
            wait_out(relay_out.at[n, k], relay_send.at[n, k])
            wait_out(fin_out.at[n, k], fin_send.at[n, k])
        wait_out(hx_out.at[n], hx_send.at[n])
        return carry

    lax.fori_loop(0, count, sent, 0)
    wait_out(relay_out.at[LOW, 0], relay_send.at[LOW, 0])
    for way in range(2):
        wait_out(fin_out.at[LOW, way, 0], fin_send.at[LOW, way])

    @pl.when(h == 1)
    def _():
        wait_out(hx_out.at[LOW], hx_send.at[LOW])

    wait_out(info_in.at[pl.ds(1, NOCC - 1)], tail_send.at[0])
    wait_out(first_in.at[pl.ds(1, 7)], tail_send.at[1])

    wait_in(all_in.at[pl.ds(1, NOCC - 1)], tail_recv.at[2])
    for k, _, _, from_row in others:
        picked += jnp.where(wanted == from_row * VB + lanes, all_in[k, 0:1, :], 0.0)
        total += all_in[k, 1:2, :]
    sublane = lax.broadcasted_iota(jnp.int32, (8, VB), 0)
    picked = jnp.where(sublane == 6, jnp.broadcast_to(total, (8, VB)), picked)
    out[...] = jnp.broadcast_to(jnp.sum(picked, axis=1, keepdims=True), (8, VB))
    wait_out(all_in.at[pl.ds(1, NOCC - 1)], tail_send.at[2])


def place_codes(orbital, table, live):
    partner = jnp.maximum(table[:, 0], 0)
    left = jnp.maximum(table[:, 1], 0)
    right = jnp.maximum(table[:, 2], 0)

    def split(index):
        return index // 8, index // 2 % 4, index % 2

    xi, zi, ci = split(jnp.broadcast_to(orbital, partner.shape))
    xj, zj, cj = split(partner)

    def row_at(first, second):
        found = jnp.full(first.shape, -1, jnp.int32)
        for a in range(4):
            for b in range(4):
                if ROW_AT[a][b] >= 0:
                    found = jnp.where((first == a) & (second == b), ROW_AT[a][b], found)
        return found

    direct = row_at(zi, zj)
    ahead = (xj - xi) % 4
    swap = (direct < 0) | ((zi == zj) & (ahead == 3))
    unit = jnp.where(swap, row_at(zj, zi), direct)
    dx = jnp.where(swap, (4 - ahead) % 4, ahead)
    dc = (ci + cj) % 2
    quadrant = jnp.where(swap, right * 2 + left, left * 2 + right)
    row_x, row_c = jnp.where(swap, xj, xi), jnp.where(swap, cj, ci)
    column_z = jnp.where(swap, zi, zj)
    device = (row_x * 4 + column_z) * 2 + row_c
    lane = unit * 32 + (dc * 4 + dx) * 4 + quadrant
    return jnp.where(live, device * VB + lane, -1)


def local(b_factors, occ_energies, vir_energies, pair_list, pair_count):
    table = pair_list[0]
    slot_total = table.shape[0]
    orbital = lax.axis_index(OCC).astype(jnp.int32)
    share = slot_total // 8
    live = jnp.arange(slot_total, dtype=jnp.int32) < pair_count[0]
    codes = place_codes(orbital, table, live)
    device_hot = (codes[None, :] // VB == jnp.arange(NOCC, dtype=jnp.int32)[:, None]) & live[None, :]
    lane_hot = codes[:, None] % VB == jnp.arange(VB, dtype=jnp.int32)[None, :]
    weights = jnp.dot(device_hot.astype(jnp.bfloat16), lane_hot.astype(jnp.bfloat16),
                      preferred_element_type=jnp.float32)
    sub = lax.broadcasted_iota(jnp.int32, (NOCC, 8, VB), 1)
    info = jnp.where(sub == 0, weights[:, None, :], occ_energies[0])
    mine = lax.dynamic_slice_in_dim(codes, lax.axis_index(AUX) * share, share, 0)
    mine = jnp.concatenate([mine, jnp.full((8 - share,), -1, jnp.int32)])
    mine = jnp.broadcast_to(mine[:, None], (8, VB))
    vmem = pl.BlockSpec(memory_space=pltpu.VMEM)
    bf16, f32 = jnp.bfloat16, jnp.float32
    dma = pltpu.SemaphoreType.DMA
    tile = (VB, VB)
    result = pl.pallas_call(
        kernel,
        out_shape=jax.ShapeDtypeStruct((8, VB), f32),
        in_specs=[pl.BlockSpec(memory_space=pl.ANY), vmem, vmem, vmem],
        out_specs=vmem,
        scratch_shapes=[
            pltpu.VMEM((11, *b_factors.shape[1:]), bf16),
            pltpu.VMEM((NOCC, 8, VB), f32),
            pltpu.VMEM((SLOTS, 2, 4, *tile), f32),
            pltpu.VMEM((SLOTS, 2, *tile), bf16),
            pltpu.VMEM((SLOTS, 2, *tile), bf16),
            pltpu.VMEM((SLOTS, 2, 2, *tile), bf16),
            pltpu.VMEM((SLOTS, 2, 2, *tile), bf16),
            pltpu.VMEM((SLOTS, *tile), f32),
            pltpu.VMEM((SLOTS, *tile), bf16),
            pltpu.VMEM((SLOTS, *tile), bf16),
            pltpu.VMEM(tile, f32),
            pltpu.VMEM((8, VB), f32),
            pltpu.VMEM((8, 8, VB), f32),
            pltpu.VMEM((8, VB), f32),
            pltpu.VMEM((NOCC, 8, VB), f32),
            dma, dma((6,)), dma((6,)), dma((4,)), dma((4,)), dma((3, 2)), dma((4, 2)),
            dma((SLOTS, 2)), dma((SLOTS, 2)), dma((SLOTS, 2)), dma((SLOTS, 2)),
            dma((SLOTS,)), dma((SLOTS,)), dma((3,)), dma((3,)),
        ],
        compiler_params=pltpu.CompilerParams(collective_id=0, has_side_effects=True),
        name="pair_energies",
    )(b_factors, info, mine, vir_energies.reshape(2, VB))
    return result[:share, 0][None, :], result[6, 0]


def solution(mesh):
    finer = Mesh(mesh.devices.reshape(4, 4, 2, 4, 2), NAMES)
    placed = (P(OCC, None, AUX), P(OCC), P(), P(OCC, None, None), P(OCC))
    return jax.shard_map(
        local, mesh=finer, in_specs=placed, out_specs=(P(OCC, AUX), P()), check_vma=False
    )
```

time: 494 us -> 108 us (0.22)
  waiting for transfers between devices: 367 us -> 0 us
  Pallas kernels: 0 us -> 101 us
  blocking collectives: 41.4 us -> 0 us
  local copies, waits for them, and re-layouts: 35.5 us -> 3.26 us
  between operations: 16.5 us -> 2.05 us
  matrix products: 14.1 us -> 0.19 us
  starting transfers between devices: 8.34 us -> 0 us
  other arithmetic: 8.77 us -> 0.82 us
    unnamed x5 -> x0, waiting for transfers between devices: 215 us -> none
    all_gather x1 -> x0, waiting for transfers between devices: 147 us -> none  [local(): lax.all_gather(b_factors, OCC, axis=0, tiled=True)]
    pallas_call x0 -> x1, Pallas kernels: none -> 101 us  [local(): pl.pallas_call(kernel, out_shape=jax.ShapeDtypeStruct((8, VB), f32), in_s...]
    psum x5 -> x0, blocking collectives: 41.4 us -> none  [by_axis(): array = lax.psum(array, axis)]
    reshape x2 -> x0, local copies, waits for them, and re-layouts: 18.5 us -> none  [local(): tiles = block.reshape(orbital_total, block_count, VB, block_count, VB)]
    dot_general x3 -> x1, matrix products: 14.1 us -> 0.19 us  [local(): jnp.dot(device_hot.astype(jnp.bfloat16), lane_hot.astype(jnp.bfloat16), p...]
    gather x2 -> x0, local copies, waits for them, and re-layouts: 9.92 us -> none  [the longest x1 5.8 us: local(): direct_tiles = jnp.take(tiles, direct_code, axis=0)]
    all_to_all x1 -> x0, starting transfers between devices: 8.22 us -> none  [sent_to_all(): lax.all_to_all(jnp.broadcast_to(array[None], (count, *array.shape)), axis...]
  transfers between devices with their start and end apart: 4 -> 0, of which waited for: 4 -> 0; matrix products, arithmetic and copies ran while one was open for 1% -> 0% of each run, Pallas kernels for 0% -> 0%
where the time goes in v1:
time: 108 us
  Pallas kernels  101 us (94%)
  local copies, waits for them, and re-layouts  3.26 us (3%)
  between operations  2.05 us (2%)
    pallas_call x1, Pallas kernels, local(): pl.pallas_call(kernel, out_shape=jax.ShapeDtypeStruct((8, VB), f32), in_s...  101 us
    slice x2, local copies, waits for them, and re-layouts, local(): return (result[:share, 0][None, :], result[6, 0])  2.51 us

profile of v1, /device:TPU:1, one launch (start us, length us, event | category | flops | bytes accessed | tf_op | source)
XLA Modules:
  0.0 107.8 jit_solution(18358495663365918679)
XLA Ops:
  0.7 0.0 copy-start
  1.4 0.0 copy-done
  1.5 0.2 fusion
  2.3 0.7 broadcast_select_fusion.info_out
  3.1 0.1 dynamic_slice.3
  3.1 0.7 broadcast_in_dim.50.codes
  3.8 101.5 %pair_energies.1 = f32[8,128]{1,0:T(8,128)} custom-call(bf16[1,256,1536]{2,1,0:T(8,128)(2,1)} %b_hbm.1, f32[32,8,128]{2,1,0:T(8,128)} %broadcast_select_fusion.info_out, s32[8,128]{1,0:T(8,128)} %broadcast_in_dim.50.codes, f32[2,128]{1,0:T(2,128)} %bitcast.85), custom_call_target="tpu_custom_call" | custom-call | tf_op jit(solution)/shard_map/pair_energies/pallas_call | solution.py:510
  105.3 1.2 %slice.19 = f32[1,1]{1,0:T(1,128)} slice(f32[8,128]{1,0:T(8,128)} %pair_energies.1), slice={[6:7], [0:1]} | slice | bytes 8 | tf_op jit(solution)/shard_map/slice | solution.py:538
  106.5 1.3 %slice_reduce_fusion = f32[6]{0:T(128)} fusion(f32[8,128]{1,0:T(8,128)} %pair_energies.1), kind=kLoop, calls=%fused_computation.8 | loop fusion | bytes 48 | tf_op jit(solution)/shard_map/slice | solution.py:538
  (6 shorter events, 0.1 us)
Async XLA Ops:
  0.7 0.7 copy-start

commit v2 on v1

--- a/solution.py
+++ b/solution.py
@@ -9,7 +9,7 @@
 VB = 128
 NV = 256
 NOCC = 32
-SLOTS = 16
+SLOTS = 12
 LOW = SLOTS - 1
 HALF = 128
 OCC = ("occ_0", "occ_1", "occ_2")
@@ -18,16 +18,16 @@
 MESH = pl.DeviceIdType.MESH
 
 UNITS = (
-    ((0, 0), (0, 1), (0, 2)),
+    ((0, 0), (0, 1), (0, 2), (2, 0), (2, 1), (2, 3), (2, 2)),
+    ((0, 0), (0, 1), (1, 0), (1, 1), (1, 3), (0, 2), (1, 2), (2, 0), (2, 1), (2, 3), (2, 2)),
+    ((0, 0), (0, 1), (1, 0), (1, 1), (1, 3), (0, 2), (1, 2), (2, 0), (2, 1), (2, 3), (2, 2)),
     ((0, 0), (0, 1), (1, 0), (1, 1), (1, 3), (0, 2), (1, 2)),
-    ((0, 0), (0, 1), (1, 0), (1, 1), (1, 3), (2, 0), (2, 1), (2, 3),
-     (0, 2), (1, 2), (2, 2), (3, 0), (3, 1), (3, 3), (3, 2)),
-    ((0, 0), (0, 1), (1, 0), (1, 1), (1, 3), (0, 2), (1, 2), (3, 0), (3, 1), (3, 3), (3, 2)),
 )
-COUNT = (3, 7, 15, 11)
-SECOND = (2, 5, 8, 5)
-THIRD = (3, 7, 11, 7)
-ROW_AT = ((0, 1, 3, 3), (-1, 0, 1, 1), (-1, -1, 0, -1), (-1, -1, 2, 0))
+COUNT = (7, 11, 11, 7)
+SECOND = (2, 5, 5, 5)
+THIRD = (3, 7, 7, 7)
+MOVES = ((0, 1, 1), (1, 2, 1), (2, 3, 1), (3, 1, 2), (0, 2, 2), (3, 0, 2))
+ROW_AT = ((0, 1, 2, -1), (-1, 0, 1, -1), (-1, -1, 0, 1), (2, 2, -1, 0))
 
 
 def packed(values):
@@ -41,7 +41,7 @@
 DX_TABLE = tuple(packed([dx for _, dx in row]) for row in UNITS)
 
 
-def kernel(b_hbm, info_out, codes, vir, out, panels, info_in, parts, relay_out, relay_in, fin_out, fin_in,
+def kernel(b_hbm, info_out, codes, vir, out, total_out, panels, info_in, parts, relay_out, relay_in, fin_out, fin_in,
            keep, hx_out, hx_in, vsum, acc, first_in, all_out, all_in,
            load_sem, x_send, x_recv, d_send, d_recv, z_send, z_recv, relay_send, relay_recv,
            fin_send, fin_recv, hx_send, hx_recv, tail_send, tail_recv):
@@ -113,18 +113,16 @@
     def core_copy(dx):
         return send(panels.at[dx], panels.at[4 + dx], d_send.at[dx], d_recv.at[dx], dev_core)
 
-    def z_copy(slot, to_slot, part, to_z, kind):
-        return send(half(slot, part), half(to_slot, part), z_send.at[kind, part],
-                    z_recv.at[to_slot - 7, part], (x, to_z, c, y, h))
-
-    own_z = {0: (0, 8, 1), 1: (0, 8, 2), 3: (0, 9, 2)}
+    def z_copy(to_z, u, kind):
+        return send(panels.at[0], panels.at[7 + u], z_send.at[kind], z_recv.at[u], (x, to_z, c, y, h))
+
     own_x[0].start()
     own_x[2].start()
-    for from_z, (slot, to_slot, to_z) in own_z.items():
+    for index, (from_z, to_z, u) in enumerate(MOVES):
         @pl.when(z == from_z)
-        def _(slot=slot, to_slot=to_slot, to_z=to_z):
-            z_copy(slot, to_slot, 0, to_z, 0).start()
-            z_copy(slot, to_slot, 1, to_z, 0).start()
+        def _(to_z=to_z, u=u, kind=index // 4):
+            z_copy(to_z, u, kind).start()
+
     core_copy(0).start()
     own_x[1].start()
     own_x[3].start()
@@ -254,10 +252,9 @@
                 keep[0] += hx_in[LOW].astype(jnp.float32)
 
         tile = keep[n] + hx_in[n].astype(jnp.float32)
-        u_three = u // 3
-        u_two = u // 2 - u_three
-        u_one = (u + 3) // 4 - u // 2
-        row_z = z * (1 - (u + 3) // 4) + u_one * at_least_two + u_two * 3
+        first = u % 2 * (z - 1)
+        second_row = u // 2 * (3 - 3 * (at_least_two - at_three))
+        row_z = z * (1 - (u + 1) // 2) + first + second_row
         row_energy = info_in[(row_z - z + 4) % 4 * 2][1:2, :]
         column_energy = info_in[dx * 8 + h][1:2, :]
         denominator = vsum[...] - row_energy - column_energy
@@ -278,52 +275,29 @@
             other = jnp.sum(other, axis=1, keepdims=True)
             acc[0:1, :] += jnp.where(lane_row == lane + 1, value, 0.0) + jnp.where(lane_row == lane + 2, other, 0.0)
 
-    def pass_rows(part, slot, to_slot, to_z, kind):
-        wait_in(half(slot, part), z_recv.at[slot - 7, part])
-        z_copy(slot, to_slot, part, to_z, kind).start()
-
     def first_arrivals():
         own_x[0].wait_recv()
         passed_x[0].start()
         own_x[2].wait_recv()
         passed_x[1].start()
-        for part in range(2):
-            @pl.when(z == 1)
-            def _():
-                pass_rows(part, 8, 10, 2, 1)
-
-            @pl.when(z == 2)
-            def _():
-                pass_rows(part, 8, 8, 3, 1)
-
-            if part == 0:
-                own_x[1].wait_recv()
-                core_copy(3).start()
-                own_x[3].wait_recv()
-                core_copy(1).start()
+
+    def second_arrivals():
+        own_x[1].wait_recv()
+        core_copy(3).start()
+        own_x[3].wait_recv()
+        core_copy(1).start()
         wait_in(panels.at[7], d_recv.at[3])
         wait_in(panels.at[5], d_recv.at[1])
 
-    def second_arrivals():
+        @pl.when(z >= 1)
+        def _():
+            wait_in(panels.at[8], z_recv.at[1])
+
+    def third_arrivals():
         passed_x[0].wait_recv()
         passed_x[1].wait_recv()
         core_copy(2).start()
-
-        @pl.when(z == 2)
-        def _():
-            pass_rows(0, 10, 10, 3, 2)
-
         wait_in(panels.at[6], d_recv.at[2])
-
-    def third_arrivals():
-        @pl.when(z == 2)
-        def _():
-            pass_rows(1, 10, 10, 3, 2)
-
-        @pl.when(z == 3)
-        def _():
-            for part in range(2):
-                wait_in(half(10, part), z_recv.at[3, part])
 
     def each(low, high, action):
         def one(n, carry):
@@ -340,43 +314,29 @@
         def _():
             pass_on(0)
             first_arrivals()
+            cross(0)
+            second_arrivals()
 
         @pl.when(n == second - 1)
         def _():
             each(1, second, pass_on)
-            second_arrivals()
-
-        @pl.when(n == 1)
-        def _():
-            cross(0)
-
-            @pl.when(z == 3)
+            third_arrivals()
+
+        @pl.when(n == third - 1)
+        def _():
+            each(second, third, pass_on)
+            each(1, second, cross)
+
+            @pl.when(z <= 2)
             def _():
-                for part in range(2):
-                    wait_in(half(8, part), z_recv.at[1, part])
-
-        @pl.when(n == 4)
-        def _():
-            @pl.when(z == 2)
-            def _():
-                for part in range(2):
-                    wait_in(half(9, part), z_recv.at[2, part])
-
-        @pl.when(n == third - 1)
-        def _():
-            @pl.when(z >= 2)
-            def _():
-                each(1, early, cross)
-                third_arrivals()
+                wait_in(panels.at[9], z_recv.at[2])
 
         return (u_table // 4, dx_table // 4)
 
     start = jnp.int32(0)
-    early = (second + 1) // 2
-    crossed = 1 + (early - 1) * at_least_two
     lax.fori_loop(0, count, step, (start + by_z(U_TABLE), start + by_z(DX_TABLE)))
-    each(second, count, pass_on)
-    each(crossed, count, cross)
+    each(third, count, pass_on)
+    each(second, third, cross)
     wait_in(info_in.at[pl.ds(1, NOCC - 1)], tail_recv.at[0])
 
     def finish(n, carry):
@@ -384,7 +344,9 @@
         energies(n, u_table % 4, dx_table % 4)
         return (u_table // 4, dx_table // 4)
 
-    lax.fori_loop(0, count, finish, (start + by_z(U_TABLE), start + by_z(DX_TABLE)))
+    tables = lax.fori_loop(0, second, finish, (start + by_z(U_TABLE), start + by_z(DX_TABLE)))
+    each(third, count, cross)
+    lax.fori_loop(second, count, finish, tables)
 
     for _, there, device in aux_others:
         send(acc, first_in.at[there], tail_send.at[1], tail_recv.at[1], device).start()
@@ -411,19 +373,11 @@
         passed_x[k].wait_send()
     for dx in range(4):
         core_copy(dx).wait_send()
-    for part in range(2):
-        @pl.when(z != 2)
-        def _():
-            wait_out(half(0, part), z_send.at[0, part])
-
-        @pl.when(z == 1)
-        def _():
-            wait_out(half(8, part), z_send.at[1, part])
-
-        @pl.when(z == 2)
-        def _():
-            wait_out(half(8, part), z_send.at[1, part])
-            wait_out(half(10, part), z_send.at[2, part])
+    wait_out(panels.at[0], z_send.at[0])
+
+    @pl.when(z % 3 == 0)
+    def _():
+        wait_out(panels.at[0], z_send.at[1])
 
     def sent(n, carry):
         for k in range(2):
@@ -449,8 +403,10 @@
         picked += jnp.where(wanted == from_row * VB + lanes, all_in[k, 0:1, :], 0.0)
         total += all_in[k, 1:2, :]
     sublane = lax.broadcasted_iota(jnp.int32, (8, VB), 0)
-    picked = jnp.where(sublane == 6, jnp.broadcast_to(total, (8, VB)), picked)
-    out[...] = jnp.broadcast_to(jnp.sum(picked, axis=1, keepdims=True), (8, VB))
+    picked = jnp.sum(picked, axis=1, keepdims=True)
+    picked = jnp.sum(jnp.where(sublane == lanes, picked, 0.0), axis=0, keepdims=True)
+    out[...] = picked[:, : out.shape[1]]
+    total_out[...] = jnp.sum(total, axis=1, keepdims=True)
     wait_out(all_in.at[pl.ds(1, NOCC - 1)], tail_send.at[2])
 
 
@@ -507,13 +463,13 @@
     bf16, f32 = jnp.bfloat16, jnp.float32
     dma = pltpu.SemaphoreType.DMA
     tile = (VB, VB)
-    result = pl.pallas_call(
+    pair_energy, total_energy = pl.pallas_call(
         kernel,
-        out_shape=jax.ShapeDtypeStruct((8, VB), f32),
+        out_shape=(jax.ShapeDtypeStruct((1, share), f32), jax.ShapeDtypeStruct((1, 1), f32)),
         in_specs=[pl.BlockSpec(memory_space=pl.ANY), vmem, vmem, vmem],
-        out_specs=vmem,
+        out_specs=(vmem, vmem),
         scratch_shapes=[
-            pltpu.VMEM((11, *b_factors.shape[1:]), bf16),
+            pltpu.VMEM((10, *b_factors.shape[1:]), bf16),
             pltpu.VMEM((NOCC, 8, VB), f32),
             pltpu.VMEM((SLOTS, 2, 4, *tile), f32),
             pltpu.VMEM((SLOTS, 2, *tile), bf16),
@@ -528,14 +484,14 @@
             pltpu.VMEM((8, 8, VB), f32),
             pltpu.VMEM((8, VB), f32),
             pltpu.VMEM((NOCC, 8, VB), f32),
-            dma, dma((6,)), dma((6,)), dma((4,)), dma((4,)), dma((3, 2)), dma((4, 2)),
+            dma, dma((6,)), dma((6,)), dma((4,)), dma((4,)), dma((2,)), dma((3,)),
             dma((SLOTS, 2)), dma((SLOTS, 2)), dma((SLOTS, 2)), dma((SLOTS, 2)),
             dma((SLOTS,)), dma((SLOTS,)), dma((3,)), dma((3,)),
         ],
         compiler_params=pltpu.CompilerParams(collective_id=0, has_side_effects=True),
         name="pair_energies",
     )(b_factors, info, mine, vir_energies.reshape(2, VB))
-    return result[:share, 0][None, :], result[6, 0]
+    return pair_energy, total_energy[0, 0]
 
 
 def solution(mesh):

time: 108 us -> 99.2 us (0.919)
  Pallas kernels: 101 us -> 92.4 us
  between operations: 2.05 us -> 3.74 us
  local copies, waits for them, and re-layouts: 3.26 us -> 1.87 us
    pallas_call x1, Pallas kernels: 101 us -> 92.4 us  [local(): pl.pallas_call(kernel, out_shape=(jax.ShapeDtypeStruct((1, share), f32),...]
    slice x2 -> x0, local copies, waits for them, and re-layouts: 2.51 us -> none  [local(): return (result[:share, 0][None, :], result[6, 0])]
    unnamed x3 -> x6, local copies, waits for them, and re-layouts: 0.02 us -> 1.14 us
where the time goes in v2:
time: 99.2 us; the launch traced here: 99 us
  Pallas kernels  92.4 us (93%)
  between operations  3.74 us (4%)
  local copies, waits for them, and re-layouts  1.87 us (2%)
    pallas_call x1, Pallas kernels, local(): pl.pallas_call(kernel, out_shape=(jax.ShapeDtypeStruct((1, share), f32),...  92.4 us

profile of v2, /device:TPU:1, one launch (start us, length us, event | category | flops | bytes accessed | tf_op | source)
XLA Modules:
  0.0 99.0 jit_solution(6688045670934205253)
XLA Ops:
  0.7 0.0 copy-start
  1.4 0.0 copy-done
  1.5 0.2 fusion
  2.3 0.7 broadcast_select_fusion.info_out
  3.1 0.1 dynamic_slice.3
  3.1 0.7 broadcast_in_dim.50.codes
  3.8 92.4 %pair_energies.1 = (f32[1,6]{1,0:T(1,128)}, f32[1,1]{1,0:T(1,128)}) custom-call(bf16[1,256,1536]{2,1,0:T(8,128)(2,1)} %b_hbm.1, f32[32,8,128]{2,1,0:T(8,128)} %broadcast_select_fusion.info_out, s32[8,128]{1,0:T(8,128)} %broadcast_in_dim.50.codes, f32[2,128]{1,0:T(2,128)} %bitcast.90), custom_call_target="tpu_custom_call" | custom-call | tf_op jit(solution)/shard_map/pair_energies/pallas_call | solution.py:466
  96.2 0.0 copy-start.1
  96.2 0.6 copy-done.1
  96.8 0.5 copy.14
  (6 shorter events, 0.1 us)
Async XLA Ops:
  0.7 0.7 copy-start
  96.2 0.6 copy-start.1

commit v3 on v2

--- a/solution.py
+++ b/solution.py
@@ -44,7 +44,7 @@
 def kernel(b_hbm, info_out, codes, vir, out, total_out, panels, info_in, parts, relay_out, relay_in, fin_out, fin_in,
            keep, hx_out, hx_in, vsum, acc, first_in, all_out, all_in,
            load_sem, x_send, x_recv, d_send, d_recv, z_send, z_recv, relay_send, relay_recv,
-           fin_send, fin_recv, hx_send, hx_recv, tail_send, tail_recv):
+           fin_send, fin_recv, hx_send, hx_recv, tail_send, tail_recv, turn):
     x, z, c, y, h = (lax.axis_index(name) for name in NAMES)
     me = (x * 4 + z) * 2 + c
     xs, zs, ys = ([(v + k) % 4 for k in range(4)] for v in (x, z, y))
@@ -68,10 +68,12 @@
         kx, kz, kc = k // 8, k // 2 % 4, k % 2
         there = (-kx % 4 * 4 + -kz % 4) * 2 + kc
         others.append((k, there, (xs[kx], zs[kz], cs[kc], y, h), (xs[kx] * 4 + zs[kz]) * 2 + cs[kc]))
-    aux_others = []
-    for k in range(1, 8):
-        ky, kh = k // 2, k % 2
-        aux_others.append((k, -ky % 4 * 2 + kh, (x, z, c, ys[ky], hs[kh])))
+    plane = [(k, -(k // 4) % 4 * 4 + -k % 4, (xs[k // 4], z, c, ys[k % 4], h)) for k in range(1, 16)]
+    column = [(k, (-(k // 4) % 4 * 2 + k // 2 % 2) * 2 + k % 2, (x, zs[k // 4], cs[k % 2], y, hs[k // 2 % 2]))
+              for k in range(1, 16)]
+    greeted = [device for _, _, device, _ in others] + [dev_h]
+    greeted += [device for k, _, device in plane if k % 4 != 0]
+    greeted += [device for k, _, device in column if k // 2 % 2 == 1 and k != 2]
 
     def send(src, dst, send_sem, recv_sem, device):
         return pltpu.make_async_remote_copy(
@@ -92,12 +94,10 @@
 
     barrier = pltpu.get_barrier_semaphore()
 
-    for _, _, device, _ in others:
-        pl.semaphore_signal(barrier, inc=1, device_id=device, device_id_type=MESH)
-    for _, _, device in aux_others:
+    for device in greeted:
         pl.semaphore_signal(barrier, inc=1, device_id=device, device_id_type=MESH)
     load.wait()
-    pl.semaphore_wait(barrier, NOCC - 1 + 7)
+    pl.semaphore_wait(barrier, len(greeted))
 
     own_x = (
         send(half(0, 0), half(3, 0), x_send.at[0], x_recv.at[0], dev_x[0]),
@@ -121,7 +121,12 @@
     for index, (from_z, to_z, u) in enumerate(MOVES):
         @pl.when(z == from_z)
         def _(to_z=to_z, u=u, kind=index // 4):
-            z_copy(to_z, u, kind).start()
+            if kind == 0:
+                z_copy(to_z, u, kind).start()
+            else:
+                @pl.when(c == 0)
+                def _():
+                    z_copy(to_z, u, kind).start()
 
     core_copy(0).start()
     own_x[1].start()
@@ -298,6 +303,19 @@
         passed_x[1].wait_recv()
         core_copy(2).start()
         wait_in(panels.at[6], d_recv.at[2])
+        for index, (from_z, to_z, u) in enumerate(MOVES):
+            if index // 4 == 1:
+                @pl.when(z == from_z)
+                def _(to_z=to_z, u=u):
+                    @pl.when(c == 0)
+                    def _():
+                        wait_out(panels.at[0], z_send.at[1])
+                        pl.semaphore_signal(turn, inc=1, device_id=dev_core, device_id_type=MESH)
+
+                    @pl.when(c == 1)
+                    def _():
+                        pl.semaphore_wait(turn, 1)
+                        z_copy(to_z, u, 1).start()
 
     def each(low, high, action):
         def one(n, carry):
@@ -348,24 +366,26 @@
     each(third, count, cross)
     lax.fori_loop(second, count, finish, tables)
 
-    for _, there, device in aux_others:
-        send(acc, first_in.at[there], tail_send.at[1], tail_recv.at[1], device).start()
     weights = jnp.zeros((1, VB), jnp.float32)
     for k in range(NOCC):
         weights += info_in[k, 0:1, :]
-    wait_in(first_in.at[pl.ds(1, 7)], tail_recv.at[1])
-    mine = acc[0:1, :]
-    for k in range(1, 8):
-        mine += first_in[k, 0:1, :]
-    all_out[0:1, :] = mine
-    all_out[1:2, :] = mine * weights
-
-    for _, there, device, _ in others:
+    acc[1:2, :] = acc[0:1, :] * weights
+    for _, there, device in plane:
+        send(acc, first_in.at[there], tail_send.at[1], tail_recv.at[1], device).start()
+    first_in[0] = acc[...]
+    wait_in(first_in.at[pl.ds(1, 15)], tail_recv.at[1])
+    all_out[5:8, :] = jnp.zeros((3, VB), jnp.float32)
+    total = jnp.zeros((1, VB), jnp.float32)
+    for kx in range(4):
+        both = first_in[4 * kx] + first_in[4 * kx + 1] + first_in[4 * kx + 2] + first_in[4 * kx + 3]
+        all_out[kx : kx + 1, :] = both[0:1, :]
+        total += both[1:2, :]
+    all_out[4:5, :] = total
+    for _, there, device in column:
         send(all_out, all_in.at[there], tail_send.at[2], tail_recv.at[2], device).start()
     wanted = codes[...]
     lanes = lax.broadcasted_iota(jnp.int32, (8, VB), 1)
-    picked = jnp.where(wanted == me * VB + lanes, all_out[0:1, :], 0.0)
-    total = all_out[1:2, :]
+    all_in[0] = all_out[...]
 
     for k in range(4):
         own_x[k].wait_send()
@@ -377,7 +397,9 @@
 
     @pl.when(z % 3 == 0)
     def _():
-        wait_out(panels.at[0], z_send.at[1])
+        @pl.when(c == 1)
+        def _():
+            wait_out(panels.at[0], z_send.at[1])
 
     def sent(n, carry):
         for k in range(2):
@@ -396,18 +418,24 @@
         wait_out(hx_out.at[LOW], hx_send.at[LOW])
 
     wait_out(info_in.at[pl.ds(1, NOCC - 1)], tail_send.at[0])
-    wait_out(first_in.at[pl.ds(1, 7)], tail_send.at[1])
-
-    wait_in(all_in.at[pl.ds(1, NOCC - 1)], tail_recv.at[2])
-    for k, _, _, from_row in others:
-        picked += jnp.where(wanted == from_row * VB + lanes, all_in[k, 0:1, :], 0.0)
-        total += all_in[k, 1:2, :]
+    wait_out(first_in.at[pl.ds(1, 15)], tail_send.at[1])
+
+    wait_in(all_in.at[pl.ds(1, 15)], tail_recv.at[2])
+    picked = jnp.zeros((8, VB), jnp.float32)
+    total = jnp.zeros((1, VB), jnp.float32)
+    for kz in range(4):
+        for kc in range(2):
+            both = all_in[4 * kz + kc] + all_in[4 * kz + 2 + kc]
+            total += both[4:5, :]
+            for kx in range(4):
+                from_row = (xs[kx] * 4 + zs[kz]) * 2 + cs[kc]
+                picked += jnp.where(wanted == from_row * VB + lanes, both[kx : kx + 1, :], 0.0)
     sublane = lax.broadcasted_iota(jnp.int32, (8, VB), 0)
     picked = jnp.sum(picked, axis=1, keepdims=True)
     picked = jnp.sum(jnp.where(sublane == lanes, picked, 0.0), axis=0, keepdims=True)
     out[...] = picked[:, : out.shape[1]]
     total_out[...] = jnp.sum(total, axis=1, keepdims=True)
-    wait_out(all_in.at[pl.ds(1, NOCC - 1)], tail_send.at[2])
+    wait_out(all_in.at[pl.ds(1, 15)], tail_send.at[2])
 
 
 def place_codes(orbital, table, live):
@@ -454,7 +482,7 @@
     lane_hot = codes[:, None] % VB == jnp.arange(VB, dtype=jnp.int32)[None, :]
     weights = jnp.dot(device_hot.astype(jnp.bfloat16), lane_hot.astype(jnp.bfloat16),
                       preferred_element_type=jnp.float32)
-    sub = lax.broadcasted_iota(jnp.int32, (NOCC, 8, VB), 1)
+    sub = lax.broadcasted_iota(jnp.int32, (NOCC, 2, VB), 1)
     info = jnp.where(sub == 0, weights[:, None, :], occ_energies[0])
     mine = lax.dynamic_slice_in_dim(codes, lax.axis_index(AUX) * share, share, 0)
     mine = jnp.concatenate([mine, jnp.full((8 - share,), -1, jnp.int32)])
@@ -470,7 +498,7 @@
         out_specs=(vmem, vmem),
         scratch_shapes=[
             pltpu.VMEM((10, *b_factors.shape[1:]), bf16),
-            pltpu.VMEM((NOCC, 8, VB), f32),
+            pltpu.VMEM((NOCC, 2, VB), f32),
             pltpu.VMEM((SLOTS, 2, 4, *tile), f32),
             pltpu.VMEM((SLOTS, 2, *tile), bf16),
             pltpu.VMEM((SLOTS, 2, *tile), bf16),
@@ -480,13 +508,13 @@
             pltpu.VMEM((SLOTS, *tile), bf16),
             pltpu.VMEM((SLOTS, *tile), bf16),
             pltpu.VMEM(tile, f32),
+            pltpu.VMEM((2, VB), f32),
+            pltpu.VMEM((16, 2, VB), f32),
             pltpu.VMEM((8, VB), f32),
-            pltpu.VMEM((8, 8, VB), f32),
-            pltpu.VMEM((8, VB), f32),
-            pltpu.VMEM((NOCC, 8, VB), f32),
+            pltpu.VMEM((16, 8, VB), f32),
             dma, dma((6,)), dma((6,)), dma((4,)), dma((4,)), dma((2,)), dma((3,)),
             dma((SLOTS, 2)), dma((SLOTS, 2)), dma((SLOTS, 2)), dma((SLOTS, 2)),
-            dma((SLOTS,)), dma((SLOTS,)), dma((3,)), dma((3,)),
+            dma((SLOTS,)), dma((SLOTS,)), dma((3,)), dma((3,)), pltpu.SemaphoreType.REGULAR,
         ],
         compiler_params=pltpu.CompilerParams(collective_id=0, has_side_effects=True),
         name="pair_energies",

time: 99.2 us -> 88.3 us (0.89)
  Pallas kernels: 92.4 us -> 81.4 us
    pallas_call x1, Pallas kernels: 92.4 us -> 81.4 us  [local(): pl.pallas_call(kernel, out_shape=(jax.ShapeDtypeStruct((1, share), f32),...]
where the time goes in v3:
time: 88.3 us; the launch traced here: 88.1 us
  Pallas kernels  81.4 us (92%)
  between operations  3.74 us (4%)
  local copies, waits for them, and re-layouts  1.95 us (2%)
    pallas_call x1, Pallas kernels, local(): pl.pallas_call(kernel, out_shape=(jax.ShapeDtypeStruct((1, share), f32),...  81.4 us

profile of v3, /device:TPU:1, one launch (start us, length us, event | category | flops | bytes accessed | tf_op | source)
XLA Modules:
  0.0 88.1 jit_solution(10663724267351324108)
XLA Ops:
  0.7 0.0 copy-start
  1.4 0.0 copy-done
  1.5 0.2 fusion
  2.3 0.7 broadcast_select_fusion.info_out
  3.0 0.1 dynamic_slice.3
  3.1 0.7 broadcast_in_dim.50.codes
  3.8 81.4 %pair_energies.1 = (f32[1,6]{1,0:T(1,128)}, f32[1,1]{1,0:T(1,128)}) custom-call(bf16[1,256,1536]{2,1,0:T(8,128)(2,1)} %b_hbm.1, f32[32,2,128]{2,1,0:T(2,128)} %broadcast_select_fusion.info_out, s32[8,128]{1,0:T(8,128)} %broadcast_in_dim.50.codes, f32[2,128]{1,0:T(2,128)} %bitcast.90), custom_call_target="tpu_custom_call" | custom-call | tf_op jit(solution)/shard_map/pair_energies/pallas_call | solution.py:494
  85.2 0.0 copy-start.1
  85.2 0.7 copy-done.1
  85.9 0.5 copy.14
  (6 shorter events, 0.1 us)
Async XLA Ops:
  0.7 0.7 copy-start
  85.2 0.7 copy-start.1

commit v4 on v3

--- a/solution.py
+++ b/solution.py
@@ -41,10 +41,36 @@
 DX_TABLE = tuple(packed([dx for _, dx in row]) for row in UNITS)
 
 
-def kernel(b_hbm, info_out, codes, vir, out, total_out, panels, info_in, parts, relay_out, relay_in, fin_out, fin_in,
+def place_codes(x, z, c, partner, left, right, live):
+    partner, left, right = (jnp.maximum(v, 0) for v in (partner, left, right))
+    xj, zj, cj = partner >> 3, (partner >> 1) & 3, partner & 1
+    xi, zi, ci = (jnp.full(partner.shape, v, jnp.int32) for v in (x, z, c))
+
+    def row_at(first, second):
+        key = first * 4 + second
+        found = jnp.full(key.shape, -1, jnp.int32)
+        for a in range(4):
+            for b in range(4):
+                if ROW_AT[a][b] >= 0:
+                    found = jnp.where(key == a * 4 + b, ROW_AT[a][b], found)
+        return found
+
+    direct = row_at(zi, zj)
+    ahead = (xj - xi) & 3
+    swap = (direct < 0) | ((zi == zj) & (ahead == 3))
+    unit = jnp.where(swap, row_at(zj, zi), direct)
+    dx = jnp.where(swap, (4 - ahead) & 3, ahead)
+    dc = (ci + cj) & 1
+    quadrant = jnp.where(swap, right * 2 + left, left * 2 + right)
+    device = (jnp.where(swap, xj, xi) * 4 + jnp.where(swap, zi, zj)) * 2 + jnp.where(swap, cj, ci)
+    lane = unit * 32 + (dc * 4 + dx) * 4 + quadrant
+    return jnp.where(live, device * VB + lane, -1)
+
+
+def kernel(b_hbm, energy, items, listed, vir, out, total_out, panels, info_out, info_in, parts, relay_out, relay_in, fin_out, fin_in,
            keep, hx_out, hx_in, vsum, acc, first_in, all_out, all_in,
            load_sem, x_send, x_recv, d_send, d_recv, z_send, z_recv, relay_send, relay_recv,
-           fin_send, fin_recv, hx_send, hx_recv, tail_send, tail_recv, turn):
+           fin_send, fin_recv, hx_send, hx_recv, tail_send, tail_recv, turn, calm):
     x, z, c, y, h = (lax.axis_index(name) for name in NAMES)
     me = (x * 4 + z) * 2 + c
     xs, zs, ys = ([(v + k) % 4 for k in range(4)] for v in (x, z, y))
@@ -132,6 +158,22 @@
     own_x[1].start()
     own_x[3].start()
 
+    slots = items.shape[2]
+    slot_of = lax.broadcasted_iota(jnp.int32, (1, slots), 1)
+    codes = place_codes(x, z, c, items[0], items[1], items[2], slot_of < listed[...])
+    device_hot = lax.broadcasted_iota(jnp.int32, (NOCC, slots), 0) == codes >> 7
+    lane_hot = (lax.broadcasted_iota(jnp.int32, (VB, slots), 0) == codes & (VB - 1)) & (codes >= 0)
+    hits = lax.dot_general(device_hot.astype(jnp.float32).astype(jnp.bfloat16),
+                           lane_hot.astype(jnp.float32).astype(jnp.bfloat16),
+                           (((1,), (1,)), ((), ())), preferred_element_type=jnp.float32)
+    for k in range(NOCC):
+        info_out[k, 0:1, :] = hits[k : k + 1, :]
+        info_out[k, 1:2, :] = jnp.broadcast_to(energy[...], (1, VB))
+    share = out.shape[1]
+    sublane = lax.broadcasted_iota(jnp.int32, (8, slots), 0)
+    mine = lax.broadcasted_iota(jnp.int32, (8, slots), 1) == (y * 2 + h) * share + sublane
+    wanted = jnp.max(jnp.where(mine & (sublane < share), codes, -1), axis=1, keepdims=True)
+
     for _, there, device, index in others:
         send(info_out.at[index], info_in.at[there], tail_send.at[0], tail_recv.at[0], device).start()
     info_in[0] = info_out[me]
@@ -141,8 +183,8 @@
 
     row_of = lax.broadcasted_iota(jnp.int32, (VB, VB), 0)
     lane_of = lax.broadcasted_iota(jnp.int32, (VB, VB), 1)
-    left = vir[0:1, :]
-    right = vir[1:2, :]
+    left = vir[0]
+    right = vir[1]
 
     def as_column(row_values, shift):
         wide = jnp.broadcast_to(row_values, (VB, VB))
@@ -343,18 +385,27 @@
         @pl.when(n == third - 1)
         def _():
             each(second, third, pass_on)
-            each(1, second, cross)
 
             @pl.when(z <= 2)
             def _():
                 wait_in(panels.at[9], z_recv.at[2])
 
+            @pl.when(z == 2)
+            def _():
+                for to_z in (1, 3):
+                    pl.semaphore_signal(calm, inc=1, device_id=(x, to_z, c, y, h), device_id_type=MESH)
+
         return (u_table // 4, dx_table // 4)
 
     start = jnp.int32(0)
     lax.fori_loop(0, count, step, (start + by_z(U_TABLE), start + by_z(DX_TABLE)))
+
+    @pl.when(z % 2 == 1)
+    def _():
+        pl.semaphore_wait(calm, 1)
+
+    each(1, third, cross)
     each(third, count, pass_on)
-    each(second, third, cross)
     wait_in(info_in.at[pl.ds(1, NOCC - 1)], tail_recv.at[0])
 
     def finish(n, carry):
@@ -362,9 +413,8 @@
         energies(n, u_table % 4, dx_table % 4)
         return (u_table // 4, dx_table // 4)
 
-    tables = lax.fori_loop(0, second, finish, (start + by_z(U_TABLE), start + by_z(DX_TABLE)))
     each(third, count, cross)
-    lax.fori_loop(second, count, finish, tables)
+    lax.fori_loop(0, count, finish, (start + by_z(U_TABLE), start + by_z(DX_TABLE)))
 
     weights = jnp.zeros((1, VB), jnp.float32)
     for k in range(NOCC):
@@ -383,7 +433,6 @@
     all_out[4:5, :] = total
     for _, there, device in column:
         send(all_out, all_in.at[there], tail_send.at[2], tail_recv.at[2], device).start()
-    wanted = codes[...]
     lanes = lax.broadcasted_iota(jnp.int32, (8, VB), 1)
     all_in[0] = all_out[...]
 
@@ -429,7 +478,7 @@
             total += both[4:5, :]
             for kx in range(4):
                 from_row = (xs[kx] * 4 + zs[kz]) * 2 + cs[kc]
-                picked += jnp.where(wanted == from_row * VB + lanes, both[kx : kx + 1, :], 0.0)
+                picked += jnp.where(jnp.broadcast_to(wanted, (8, VB)) == from_row * VB + lanes, both[kx : kx + 1, :], 0.0)
     sublane = lax.broadcasted_iota(jnp.int32, (8, VB), 0)
     picked = jnp.sum(picked, axis=1, keepdims=True)
     picked = jnp.sum(jnp.where(sublane == lanes, picked, 0.0), axis=0, keepdims=True)
@@ -438,55 +487,9 @@
     wait_out(all_in.at[pl.ds(1, 15)], tail_send.at[2])
 
 
-def place_codes(orbital, table, live):
-    partner = jnp.maximum(table[:, 0], 0)
-    left = jnp.maximum(table[:, 1], 0)
-    right = jnp.maximum(table[:, 2], 0)
-
-    def split(index):
-        return index // 8, index // 2 % 4, index % 2
-
-    xi, zi, ci = split(jnp.broadcast_to(orbital, partner.shape))
-    xj, zj, cj = split(partner)
-
-    def row_at(first, second):
-        found = jnp.full(first.shape, -1, jnp.int32)
-        for a in range(4):
-            for b in range(4):
-                if ROW_AT[a][b] >= 0:
-                    found = jnp.where((first == a) & (second == b), ROW_AT[a][b], found)
-        return found
-
-    direct = row_at(zi, zj)
-    ahead = (xj - xi) % 4
-    swap = (direct < 0) | ((zi == zj) & (ahead == 3))
-    unit = jnp.where(swap, row_at(zj, zi), direct)
-    dx = jnp.where(swap, (4 - ahead) % 4, ahead)
-    dc = (ci + cj) % 2
-    quadrant = jnp.where(swap, right * 2 + left, left * 2 + right)
-    row_x, row_c = jnp.where(swap, xj, xi), jnp.where(swap, cj, ci)
-    column_z = jnp.where(swap, zi, zj)
-    device = (row_x * 4 + column_z) * 2 + row_c
-    lane = unit * 32 + (dc * 4 + dx) * 4 + quadrant
-    return jnp.where(live, device * VB + lane, -1)
-
-
 def local(b_factors, occ_energies, vir_energies, pair_list, pair_count):
-    table = pair_list[0]
-    slot_total = table.shape[0]
-    orbital = lax.axis_index(OCC).astype(jnp.int32)
+    slot_total = pair_list.shape[1]
     share = slot_total // 8
-    live = jnp.arange(slot_total, dtype=jnp.int32) < pair_count[0]
-    codes = place_codes(orbital, table, live)
-    device_hot = (codes[None, :] // VB == jnp.arange(NOCC, dtype=jnp.int32)[:, None]) & live[None, :]
-    lane_hot = codes[:, None] % VB == jnp.arange(VB, dtype=jnp.int32)[None, :]
-    weights = jnp.dot(device_hot.astype(jnp.bfloat16), lane_hot.astype(jnp.bfloat16),
-                      preferred_element_type=jnp.float32)
-    sub = lax.broadcasted_iota(jnp.int32, (NOCC, 2, VB), 1)
-    info = jnp.where(sub == 0, weights[:, None, :], occ_energies[0])
-    mine = lax.dynamic_slice_in_dim(codes, lax.axis_index(AUX) * share, share, 0)
-    mine = jnp.concatenate([mine, jnp.full((8 - share,), -1, jnp.int32)])
-    mine = jnp.broadcast_to(mine[:, None], (8, VB))
     vmem = pl.BlockSpec(memory_space=pltpu.VMEM)
     bf16, f32 = jnp.bfloat16, jnp.float32
     dma = pltpu.SemaphoreType.DMA
@@ -494,10 +497,11 @@
     pair_energy, total_energy = pl.pallas_call(
         kernel,
         out_shape=(jax.ShapeDtypeStruct((1, share), f32), jax.ShapeDtypeStruct((1, 1), f32)),
-        in_specs=[pl.BlockSpec(memory_space=pl.ANY), vmem, vmem, vmem],
+        in_specs=[pl.BlockSpec(memory_space=pl.ANY), vmem, vmem, vmem, vmem],
         out_specs=(vmem, vmem),
         scratch_shapes=[
             pltpu.VMEM((10, *b_factors.shape[1:]), bf16),
+            pltpu.VMEM((NOCC, 2, VB), f32),
             pltpu.VMEM((NOCC, 2, VB), f32),
             pltpu.VMEM((SLOTS, 2, 4, *tile), f32),
             pltpu.VMEM((SLOTS, 2, *tile), bf16),
@@ -515,10 +519,12 @@
             dma, dma((6,)), dma((6,)), dma((4,)), dma((4,)), dma((2,)), dma((3,)),
             dma((SLOTS, 2)), dma((SLOTS, 2)), dma((SLOTS, 2)), dma((SLOTS, 2)),
             dma((SLOTS,)), dma((SLOTS,)), dma((3,)), dma((3,)), pltpu.SemaphoreType.REGULAR,
+            pltpu.SemaphoreType.REGULAR,
         ],
         compiler_params=pltpu.CompilerParams(collective_id=0, has_side_effects=True),
         name="pair_energies",
-    )(b_factors, info, mine, vir_energies.reshape(2, VB))
+    )(b_factors, occ_energies.reshape(1, 1), jnp.transpose(pair_list, (2, 0, 1)), pair_count.reshape(1, 1),
+      vir_energies.reshape(2, 1, VB))
     return pair_energy, total_energy[0, 0]
 
 

time: 88.3 us -> 83.9 us (0.950)
  Pallas kernels: 81.4 us -> 78.9 us
    pallas_call x1, Pallas kernels: 81.4 us -> 78.9 us  [local(): pl.pallas_call(kernel, out_shape=(jax.ShapeDtypeStruct((1, share), f32),...]
where the time goes in v4:
time: 83.9 us; the launch traced here: 83.7 us
  Pallas kernels  78.9 us (94%)
  between operations  3.7 us (4%)
  local copies, waits for them, and re-layouts  1.13 us (1%)
    pallas_call x1, Pallas kernels, local(): pl.pallas_call(kernel, out_shape=(jax.ShapeDtypeStruct((1, share), f32),...  78.9 us

profile of v4, /device:TPU:1, one launch (start us, length us, event | category | flops | bytes accessed | tf_op | source)
XLA Modules:
  0.0 83.7 jit_solution(14941657119416279189)
XLA Ops:
  1.9 78.9 %pair_energies.1 = (f32[1,6]{1,0:T(1,128)}, f32[1,1]{1,0:T(1,128)}) custom-call(bf16[1,256,1536]{2,1,0:T(8,128)(2,1)} %b_hbm.1, f32[1,1]{1,0:T(1,128)} %bitcast.5.energy, s32[3,1,48]{2,1,0:T(1,128)} %bitcast.7, s32[1,1]{1,0:T(1,128)} %bitcast.6.listed, f32[2,1,128]{2,1,0:T(1,128)} %bitcast.8), custom_call_target="tpu_custom_call" | custom-call | tf_op jit(solution)/shard_map/pair_energies/pallas_call | solution.py:497
  80.8 0.0 copy-start
  80.8 0.6 copy-done
  81.5 0.5 copy.11
Async XLA Ops:
  80.8 0.6 copy-start

commit v5 on v4

--- a/solution.py
+++ b/solution.py
@@ -120,7 +120,7 @@
 
     barrier = pltpu.get_barrier_semaphore()
 
-    for device in greeted:
+    for device in reversed(greeted):
         pl.semaphore_signal(barrier, inc=1, device_id=device, device_id_type=MESH)
     load.wait()
     pl.semaphore_wait(barrier, len(greeted))
@@ -142,8 +142,6 @@
     def z_copy(to_z, u, kind):
         return send(panels.at[0], panels.at[7 + u], z_send.at[kind], z_recv.at[u], (x, to_z, c, y, h))
 
-    own_x[0].start()
-    own_x[2].start()
     for index, (from_z, to_z, u) in enumerate(MOVES):
         @pl.when(z == from_z)
         def _(to_z=to_z, u=u, kind=index // 4):
@@ -154,6 +152,8 @@
                 def _():
                     z_copy(to_z, u, kind).start()
 
+    own_x[0].start()
+    own_x[2].start()
     core_copy(0).start()
     own_x[1].start()
     own_x[3].start()
@@ -341,10 +341,6 @@
             wait_in(panels.at[8], z_recv.at[1])
 
     def third_arrivals():
-        passed_x[0].wait_recv()
-        passed_x[1].wait_recv()
-        core_copy(2).start()
-        wait_in(panels.at[6], d_recv.at[2])
         for index, (from_z, to_z, u) in enumerate(MOVES):
             if index // 4 == 1:
                 @pl.when(z == from_z)
@@ -358,6 +354,10 @@
                     def _():
                         pl.semaphore_wait(turn, 1)
                         z_copy(to_z, u, 1).start()
+        passed_x[0].wait_recv()
+        passed_x[1].wait_recv()
+        core_copy(2).start()
+        wait_in(panels.at[6], d_recv.at[2])
 
     def each(low, high, action):
         def one(n, carry):
@@ -404,8 +404,9 @@
     def _():
         pl.semaphore_wait(calm, 1)
 
-    each(1, third, cross)
+    each(1, second, cross)
     each(third, count, pass_on)
+    each(second, third, cross)
     wait_in(info_in.at[pl.ds(1, NOCC - 1)], tail_recv.at[0])
 
     def finish(n, carry):
@@ -413,12 +414,12 @@
         energies(n, u_table % 4, dx_table % 4)
         return (u_table // 4, dx_table // 4)
 
-    each(third, count, cross)
-    lax.fori_loop(0, count, finish, (start + by_z(U_TABLE), start + by_z(DX_TABLE)))
-
     weights = jnp.zeros((1, VB), jnp.float32)
     for k in range(NOCC):
         weights += info_in[k, 0:1, :]
+    each(third, count, cross)
+    lax.fori_loop(0, count, finish, (start + by_z(U_TABLE), start + by_z(DX_TABLE)))
+
     acc[1:2, :] = acc[0:1, :] * weights
     for _, there, device in plane:
         send(acc, first_in.at[there], tail_send.at[1], tail_recv.at[1], device).start()

time: 83.9 us -> 82.3 us (0.981)
  Pallas kernels: 78.9 us -> 77.3 us
    pallas_call x1, Pallas kernels: 78.9 us -> 77.3 us  [local(): pl.pallas_call(kernel, out_shape=(jax.ShapeDtypeStruct((1, share), f32),...]
where the time goes in v5:
time: 82.3 us; the launch traced here: 82.1 us
  Pallas kernels  77.3 us (94%)
  between operations  3.7 us (4%)
  local copies, waits for them, and re-layouts  1.13 us (1%)
    pallas_call x1, Pallas kernels, local(): pl.pallas_call(kernel, out_shape=(jax.ShapeDtypeStruct((1, share), f32),...  77.3 us

profile of v5, /device:TPU:1, one launch (start us, length us, event | category | flops | bytes accessed | tf_op | source)
XLA Modules:
  0.0 82.1 jit_solution(2965747260672758617)
XLA Ops:
  1.9 77.3 %pair_energies.1 = (f32[1,6]{1,0:T(1,128)}, f32[1,1]{1,0:T(1,128)}) custom-call(bf16[1,256,1536]{2,1,0:T(8,128)(2,1)} %b_hbm.1, f32[1,1]{1,0:T(1,128)} %bitcast.5.energy, s32[3,1,48]{2,1,0:T(1,128)} %bitcast.7, s32[1,1]{1,0:T(1,128)} %bitcast.6.listed, f32[2,1,128]{2,1,0:T(1,128)} %bitcast.8), custom_call_target="tpu_custom_call" | custom-call | tf_op jit(solution)/shard_map/pair_energies/pallas_call | solution.py:498
  79.2 0.0 copy-start
  79.2 0.6 copy-done
  79.8 0.5 copy.11
Async XLA Ops:
  79.2 0.6 copy-start

commit v6 on v5

--- a/solution.py
+++ b/solution.py
@@ -68,7 +68,7 @@
 
 
 def kernel(b_hbm, energy, items, listed, vir, out, total_out, panels, info_out, info_in, parts, relay_out, relay_in, fin_out, fin_in,
-           keep, hx_out, hx_in, vsum, acc, first_in, all_out, all_in,
+           keep, hx_out, hx_in, vsum, sums, spots, acc, first_in, all_out, all_in,
            load_sem, x_send, x_recv, d_send, d_recv, z_send, z_recv, relay_send, relay_recv,
            fin_send, fin_recv, hx_send, hx_recv, tail_send, tail_recv, turn, calm):
     x, z, c, y, h = (lax.axis_index(name) for name in NAMES)
@@ -177,7 +177,8 @@
     for _, there, device, index in others:
         send(info_out.at[index], info_in.at[there], tail_send.at[0], tail_recv.at[0], device).start()
     info_in[0] = info_out[me]
-    acc[...] = jnp.zeros_like(acc)
+    sums[...] = jnp.zeros_like(sums)
+    spots[...] = jnp.zeros_like(spots)
 
     wait_in(panels.at[4], d_recv.at[0])
 
@@ -310,17 +311,18 @@
         @pl.when(y < 2)
         def _():
             value = -jnp.sum(tile * (2.0 * tile - tile.T) / denominator, axis=0, keepdims=True)
-            value = jnp.sum(value, axis=1, keepdims=True)
-            acc[0:1, :] += jnp.where(lane_row == lane + 3 * y, value, 0.0)
+            sums[pl.ds(n, 1), :] = value
+            spots[pl.ds(n, 1), :] = jnp.where(lane_row == lane + 3 * y, 1.0, 0.0)
 
         @pl.when(y >= 2)
         def _():
             top, bottom, under = tile[:64], tile[64:], denominator[:64]
             value = -jnp.sum(top * (2.0 * top - bottom) / under, axis=0, keepdims=True)
             other = -jnp.sum(bottom * (2.0 * bottom - top) / under, axis=0, keepdims=True)
-            value = jnp.sum(value, axis=1, keepdims=True)
-            other = jnp.sum(other, axis=1, keepdims=True)
-            acc[0:1, :] += jnp.where(lane_row == lane + 1, value, 0.0) + jnp.where(lane_row == lane + 2, other, 0.0)
+            sums[pl.ds(n, 1), :] = value
+            sums[pl.ds(n + SLOTS, 1), :] = other
+            spots[pl.ds(n, 1), :] = jnp.where(lane_row == lane + 1, 1.0, 0.0)
+            spots[pl.ds(n + SLOTS, 1), :] = jnp.where(lane_row == lane + 2, 1.0, 0.0)
 
     def first_arrivals():
         own_x[0].wait_recv()
@@ -420,7 +422,10 @@
     each(third, count, cross)
     lax.fori_loop(0, count, finish, (start + by_z(U_TABLE), start + by_z(DX_TABLE)))
 
-    acc[1:2, :] = acc[0:1, :] * weights
+    values = jnp.sum(sums[...], axis=1, keepdims=True)
+    found = jnp.sum(spots[...] * values, axis=0, keepdims=True)
+    acc[0:1, :] = found
+    acc[1:2, :] = found * weights
     for _, there, device in plane:
         send(acc, first_in.at[there], tail_send.at[1], tail_recv.at[1], device).start()
     first_in[0] = acc[...]
@@ -513,6 +518,8 @@
             pltpu.VMEM((SLOTS, *tile), bf16),
             pltpu.VMEM((SLOTS, *tile), bf16),
             pltpu.VMEM(tile, f32),
+            pltpu.VMEM((2 * SLOTS, VB), f32),
+            pltpu.VMEM((2 * SLOTS, VB), f32),
             pltpu.VMEM((2, VB), f32),
             pltpu.VMEM((16, 2, VB), f32),
             pltpu.VMEM((8, VB), f32),

time: 82.3 us -> 82.3 us (level)
  no operation moved by 1% of the time
where the time goes in v6:
time: 82.3 us; the launch traced here: 82.1 us
  Pallas kernels  77.3 us (94%)
  between operations  3.7 us (4%)
  local copies, waits for them, and re-layouts  1.13 us (1%)
    pallas_call x1, Pallas kernels, local(): pl.pallas_call(kernel, out_shape=(jax.ShapeDtypeStruct((1, share), f32),...  77.3 us

profile of v6, /device:TPU:1, one launch (start us, length us, event | category | flops | bytes accessed | tf_op | source)
XLA Modules:
  0.0 82.1 jit_solution(1523769393106123512)
XLA Ops:
  1.9 77.3 %pair_energies.1 = (f32[1,6]{1,0:T(1,128)}, f32[1,1]{1,0:T(1,128)}) custom-call(bf16[1,256,1536]{2,1,0:T(8,128)(2,1)} %b_hbm.1, f32[1,1]{1,0:T(1,128)} %bitcast.5.energy, s32[3,1,48]{2,1,0:T(1,128)} %bitcast.7, s32[1,1]{1,0:T(1,128)} %bitcast.6.listed, f32[2,1,128]{2,1,0:T(1,128)} %bitcast.8), custom_call_target="tpu_custom_call" | custom-call | tf_op jit(solution)/shard_map/pair_energies/pallas_call | solution.py:503
  79.2 0.0 copy-start
  79.2 0.6 copy-done
  79.9 0.5 copy.11
Async XLA Ops:
  79.2 0.6 copy-start
